TPU v7x, 512 devices: a whole 4x4x16 slice. The times are simulated.
512 devices in a mesh: query: 4 (over x), cand: 32 (over z_hi, y, core), tensor: 4 (over z_lo).
Axes of the slice: x: 4, y: 4, z: 16 (z_hi: 4, z_lo: 4; z = z_hi * 4 + z_lo), core: 2. Of those that a mesh axis runs over, the one named last changes fastest.
Arguments:
- cand_states: bfloat16 [131072, 2048], P(('query', 'cand'), 'tensor'), parts along dimension 0, may hold values from -6 to 6
- prefix_states: bfloat16 [256, 2048], P(('query', 'cand'), 'tensor'), parts along dimension 0, may hold values from -6 to 6
- norm_gain: float32 [2048], replicated, may hold values from 0.5 to 1.5
- w_query: bfloat16 [2048, 1024], P(None, 'tensor'), may hold values from -1 to 1
- w_key: bfloat16 [2048, 256], P(None, 'tensor'), may hold values from -1 to 1
- w_value: bfloat16 [2048, 256], P(None, 'tensor'), may hold values from -0.125 to 0.125
- w_out: bfloat16 [1024, 2048], P('tensor'), may hold values from -1.5 to 1.5
- cand_lengths: int32 [1024], P(('query', 'cand')), parts along dimension 0, may hold values from 32 to 128, as said below
Outputs:
- attn_out: bfloat16 [131072, 2048], P(('query', 'cand', 'tensor')), parts along dimension 0
There are 4 independent parts, one for each index of `query`. A program takes and returns all parts, laid end to end along the dimension named above; an argument that names none is the same for every part. Nothing has to cross between parts.
Inputs may be any that keep to these rules, and one draw needn't show every extreme that they name: `cand_lengths`: some candidate has all 128 slots live.
All inputs are finite; a program needn't handle non-finite values.
Results may differ from a plain program's by a relative error of at most 0.013.
Values may be sent and summed in bfloat16 or wider, within the bound.
A program may use at most 64 MiB of HBM per device.

v0:
```python
import jax
import jax.numpy as jnp
from jax import lax
from jax.sharding import PartitionSpec as P

epsilon = 1e-06
theta_base = 10000.0


def in_one_piece(arrays, axis, dim, along):
    both = jnp.concatenate(arrays, axis=along)
    filled, at, outs = (lax.all_gather(both, axis, axis=dim, tiled=True), 0, [])
    for a in arrays:
        outs.append(lax.slice_in_dim(filled, at, at + a.shape[along], axis=along))
        at += a.shape[along]
    return tuple(outs)


def joined_along(tiles, dim):
    lengths = list(tiles.shape[1:])
    lengths[dim] *= tiles.shape[0]
    return jnp.moveaxis(tiles, 0, dim).reshape(lengths)


def from_everyone(value, axis):
    copies = jnp.broadcast_to(value, (lax.axis_size(axis), *value.shape))
    return lax.all_to_all(copies, axis, split_axis=0, concat_axis=0, tiled=True)


def collect(value, axis, dim):
    return joined_along(from_everyone(value, axis), dim)


def in_one_piece_2(arrays, axis, dim, along):
    ends, at = ([], 0)
    for a in arrays[:-1]:
        at += a.shape[along]
        ends.append(at)
    both = jnp.concatenate(arrays, axis=along)
    return tuple(jnp.split(collect(both, axis, dim), ends, axis=along))


def rotate(values, positions):
    half_size = values.shape[-1] // 2
    frequency = theta_base ** (-jnp.arange(half_size, dtype=jnp.float32) * 2.0 / values.shape[-1])
    angles = positions.astype(jnp.float32)[:, None] * frequency[None, :]
    cosine = jnp.cos(angles)
    sine_part = jnp.sin(angles)
    lower_half = values[:, :half_size]
    upper_half = values[:, half_size:]
    return jnp.concatenate(
        [
            lower_half * cosine - upper_half * sine_part,
            upper_half * cosine + lower_half * sine_part,
        ],
        axis=-1,
    )


def normalize(states, norm_gain):
    values = states.astype(jnp.float32)
    square = jnp.mean(values * values, axis=-1, keepdims=True)
    return (values * lax.rsqrt(square + epsilon) * norm_gain[None, :]).astype(jnp.bfloat16)


def self_scores_of(queries, cand_keys):
    scores = jnp.einsum("cqd,ckd->cqk", queries, cand_keys, preferred_element_type=jnp.float32)
    slots = jnp.arange(scores.shape[1], dtype=jnp.int32)
    causal = slots[:, None] >= slots[None, :]
    return jnp.where(causal[None], scores, -jnp.inf)


def body(cand_states, prefix_states, norm_gain, w_query, w_key, w_value, w_out, cand_lengths):
    cand_full, prefix_full = in_one_piece((cand_states, prefix_states), "tensor", 1, 0)
    normed_cand = normalize(cand_full, norm_gain)
    normed_prefix = normalize(prefix_full, norm_gain)
    cand_count = cand_lengths.shape[0]
    cand_len = cand_full.shape[0] // cand_count
    prefix_rows = prefix_full.shape[0]
    cand_groups = lax.axis_size("cand")
    tensor_size = lax.axis_size("tensor")
    prefix_len = prefix_rows * cand_groups
    head_size = w_query.shape[1]
    cand_pos = prefix_len + jnp.tile(jnp.arange(cand_len, dtype=jnp.int32), cand_count)
    cand_key = jnp.dot(normed_cand, w_key, preferred_element_type=jnp.float32).astype(jnp.bfloat16)
    cand_value = jnp.dot(normed_cand, w_value, preferred_element_type=jnp.float32).astype(
        jnp.bfloat16
    )
    prefix_key = jnp.dot(normed_prefix, w_key, preferred_element_type=jnp.float32).astype(
        jnp.bfloat16
    )
    prefix_value = jnp.dot(normed_prefix, w_value, preferred_element_type=jnp.float32).astype(
        jnp.bfloat16
    )
    query_rows = rotate(
        jnp.dot(normed_cand, w_query, preferred_element_type=jnp.float32), cand_pos
    ) * head_size ** (-0.5)
    queries = query_rows.astype(jnp.bfloat16).reshape(cand_count, cand_len, head_size)
    cand_key, cand_value, prefix_key, prefix_value = in_one_piece_2(
        (cand_key, cand_value, prefix_key, prefix_value), "tensor", 1, 0
    )
    prefix_pos = lax.axis_index("cand") * prefix_rows + jnp.arange(prefix_rows, dtype=jnp.int32)
    prefix_key = rotate(prefix_key.astype(jnp.float32), prefix_pos).astype(jnp.bfloat16)
    cand_keys = (
        rotate(cand_key.astype(jnp.float32), cand_pos)
        .astype(jnp.bfloat16)
        .reshape(cand_count, cand_len, head_size)
    )
    cand_values = cand_value.reshape(cand_count, cand_len, head_size)
    self_scores = self_scores_of(queries, cand_keys)
    highest = self_scores.max(-1)
    weights = jnp.exp(self_scores - highest[..., None])
    highest, divisor, summed = (
        highest,
        weights.sum(-1),
        jnp.einsum(
            "cqk,ckd->cqd",
            weights.astype(jnp.bfloat16),
            cand_values,
            preferred_element_type=jnp.float32,
        ),
    )
    key_piece, value_piece = in_one_piece((prefix_key, prefix_value), "cand", 0, 1)
    prefix_scores = jnp.einsum(
        "cqd,kd->cqk", queries, key_piece, preferred_element_type=jnp.float32
    )
    new_highest = jnp.maximum(highest, prefix_scores.max(-1))
    rescale = jnp.exp(highest - new_highest)
    weights = jnp.exp(prefix_scores - new_highest[..., None])
    divisor = divisor * rescale + weights.sum(-1)
    summed = summed * rescale[..., None] + jnp.einsum(
        "cqk,kd->cqd", weights.astype(jnp.bfloat16), value_piece, preferred_element_type=jnp.float32
    )
    highest, divisor, summed = (new_highest, divisor, summed)
    slots = jnp.arange(cand_len, dtype=jnp.int32)
    live_rows = slots[None, :] < cand_lengths[:, None]
    head_rows = jnp.where(live_rows[..., None], summed / divisor[..., None], 0.0)
    head_rows = head_rows.reshape(cand_count * cand_len, head_size).astype(jnp.bfloat16)
    row_count = head_rows.shape[0] // tensor_size
    all_heads = lax.all_to_all(head_rows, "tensor", split_axis=0, concat_axis=1, tiled=True)
    full_out = lax.all_gather(w_out, "tensor", axis=0, tiled=True)
    summed_out = jnp.zeros((row_count, full_out.shape[1]), jnp.float32)
    for head_index in range(tensor_size):
        head_term = jnp.dot(
            all_heads[:, head_index * head_size : (head_index + 1) * head_size],
            full_out[head_index * head_size : (head_index + 1) * head_size],
            preferred_element_type=jnp.float32,
        )
        summed_out = summed_out + lax.optimization_barrier(head_term.astype(jnp.bfloat16)).astype(
            jnp.float32
        )
    return summed_out.astype(jnp.bfloat16)


def solution(mesh):
    in_specs = (
        P(("query", "cand"), "tensor"),
        P(("query", "cand"), "tensor"),
        P(),
        P(None, "tensor"),
        P(None, "tensor"),
        P(None, "tensor"),
        P("tensor", None),
        P(("query", "cand")),
    )
    out_specs = P(("query", "cand", "tensor"), None)
    return jax.shard_map(body, mesh=mesh, in_specs=in_specs, out_specs=out_specs, check_vma=False)
```

profile of v0, /device:TPU:1, one launch (start us, length us, event | category | flops | bytes accessed | tf_op | source)
XLA Modules:
  0.0 256.7 jit_solution(11628794614377574297)
XLA Ops:
  6.5 0.0 copy-start
  6.5 0.0 copy-start.5
  6.5 0.0 all-gather.4.cloned.1.call-start
  6.5 2.4 pad_maximum_fusion
  8.9 0.0 all-gather.4.cloned.1.call-update
  8.9 95.2 %all-gather.4.cloned.1.call-done = bf16[1026,2048]{1,0:T(8,128)(2,1)} async-done(((bf16[1026,512]{1,0:T(8,128)(2,1)}), bf16[1026,2048]{1,0:T(8,128)(2,1)}) %all-gather.4.cloned.1.call-update) | async-done | bytes 4202512 | tf_op jit(solution)/shard_map/all_gather | solution.py:12
  104.2 3.1 %fusion = f32[1024]{0:T(1024)S(1)} fusion(bf16[1026,2048]{1,0:T(8,128)(2,1)} %all-gather.4.cloned.1.call-done), kind=kLoop, calls=%fused_computation.2 | loop fusion | flops 6290432 | bytes 4198400 | tf_op jit(solution)/shard_map/reduce_sum | solution.py:62
  107.2 0.0 copy-done.5
  107.3 0.0 copy-start.4
  107.3 2.9 %fusion.2 = bf16[1024,2048]{1,0:T(8,128)(2,1)S(1)} fusion(f32[2048]{0:T(1024)S(1)} %copy-done.5, f32[1024]{0:T(1024)S(1)} %add_rsqrt_fusion, bf16[1026,2048]{1,0:T(8,128)(2,1)} %all-gather.4.cloned.1.call-done), kind=kLoop, calls=%fused_computation.4 | loop fusion | flops 8388608 | bytes 8400896 | tf_op jit(solution)/shard_map/convert_element_type | solution.py:63
  110.2 0.0 copy-done.4
  110.2 0.0 copy-start.1
  110.2 0.0 copy-start.3
  110.2 1.4 convolution_convert_fusion.4
  111.6 0.0 copy-done.3
  111.6 1.4 convolution_convert_fusion.5
  113.0 0.0 copy-done.1
  113.0 0.0 copy-start.6
  113.0 0.9 fusion.42
  113.9 1.0 convolution_convert_fusion.7
  114.9 0.1 copy.33
  115.0 1.0 convolution_convert_fusion.6
  116.0 0.1 copy.34
  116.2 0.1 concatenate.33
  116.3 1.2 broadcast_in_dim.24
  117.4 3.5 %all-to-all-start = ((bf16[4,2052,64]{1,2,0:T(8,128)(2,1)}), bf16[4,2052,64]{1,2,0:T(8,128)(2,1)S(1)}, u32[]{:S(2)}, u32[]{:S(2)}) async-start(bf16[4,2052,64]{1,2,0:T(8,128)(2,1)} %broadcast_in_dim.24), calls=%async_computation | async-start | bytes 2228224 | tf_op jit(solution)/shard_map/all_to_all | solution.py:27
  121.0 0.0 all-gather.6.cloned.1.call-start
  121.0 0.7 all-gather.6.cloned.1.call-update
  121.8 0.0 copy-done.6
  121.8 0.1 iota_compare_fusion.1
  121.9 0.0 copy-done
  121.9 4.4 %fusion.68 = f32[1024,256]{1,0:T(8,128)} fusion(bf16[1024,2048]{1,0:T(8,128)(2,1)} %copy-done.1, bf16[2048,256]{1,0:T(8,128)(2,1)S(1)} %copy-done), kind=kOutput, calls=%fused_computation.100 | convolution fusion | flops 1073741824 | bytes 6291456 | tf_op jit(solution)/shard_map/dot_general | solution.py:96
  126.3 21.3 %all-to-all-done = bf16[4,2052,64]{1,2,0:T(8,128)(2,1)S(1)} async-done(((bf16[4,2052,64]{1,2,0:T(8,128)(2,1)}), bf16[4,2052,64]{1,2,0:T(8,128)(2,1)S(1)}, u32[]{:S(2)}, u32[]{:S(2)}) %all-to-all-start) | async-done | bytes 1050656 | tf_op jit(solution)/shard_map/all_to_all | solution.py:27
  147.6 1.0 fusion.62
  148.6 0.1 bitcast_convert_fusion
  148.7 0.9 fusion.64
  149.6 0.2 copy.44
  149.8 1.2 copy.45
  151.1 0.1 fusion.63
  151.2 0.1 copy.46
  151.3 0.1 copy.47
  151.3 0.1 copy.41
  151.4 0.1 fusion.54
  151.6 65.6 %all-gather = bf16[32,2,512]{2,1,0:T(2,128)(2,1)S(1)} all-gather(bf16[1,2,512]{2,1,0:T(2,128)(2,1)S(1)} %maximum_bitcast_fusion), channel_id=1, replica_groups=mesh['query'=4,'cand'=32,'tensor'=4] {'cand'}, dimensions={0}, use_global_device_ids=true | all-gather | bytes 67584 | tf_op jit(solution)/shard_map/all_gather | solution.py:12
  217.2 1.1 copy.48
  218.4 3.8 %fusion.22 = (bf16[1024,128]{1,0:T(8,128)(2,1)S(1)}, bf16[1024,128]{1,0:T(8,128)(2,1)S(1)}, f32[1024,128]{1,0:T(8,128)S(1)}, f32[1024,128]{1,0:T(8,128)S(1)}) fusion(f32[1024,128]{1,0:T(8,128)S(1)} %copy.45, f32[1024,128]{1,0:T(8,128)S(1)} %copy.44, f32[128]{0:T(128)S(1)} %multiply_power_fusion, f32[1024]{0:T(1024)S(1)} %convert_bitcast_fusion, ...), kind=kLoop, calls=%fused_computation.40 | loop fusion | flops 1966080 | bytes 3674624 | tf_op jit(solution)/shard_map/convert.7
  222.2 0.3 fusion.67
  222.5 0.3 fusion.66
  222.8 0.1 fusion.33
  222.9 0.1 fusion.29
  223.0 0.4 convolution_multiply_fusion
  223.4 0.4 fusion.5
  223.8 1.0 copy.42
  224.8 4.7 %all-to-all-start.1 = ((bf16[4,256,256]{1,2,0:T(8,128)(2,1)}), bf16[4,256,256]{1,2,0:T(8,128)(2,1)S(1)}, u32[]{:S(2)}, u32[]{:S(2)}) async-start(bf16[4,256,256]{1,2,0:T(8,128)(2,1)} %copy.42), calls=%async_computation.1 | async-start | bytes 1048576 | tf_op jit(solution)/shard_map/all_to_all | solution.py:140
  229.5 0.0 all-gather.6.cloned.1.call-done
  229.5 14.1 %all-to-all-done.1 = bf16[4,256,256]{1,2,0:T(8,128)(2,1)S(1)} async-done(((bf16[4,256,256]{1,2,0:T(8,128)(2,1)}), bf16[4,256,256]{1,2,0:T(8,128)(2,1)S(1)}, u32[]{:S(2)}, u32[]{:S(2)}) %all-to-all-start.1) | async-done | bytes 524320 | tf_op jit(solution)/shard_map/all_to_all | solution.py:140
  243.7 0.0 copy-start.2
  243.7 1.8 convolution_convert_fusion.3
  245.5 1.7 convolution_convert_fusion.2
  247.2 0.0 copy-done.2
  247.2 0.5 convolution_convert_fusion.1
  247.7 0.5 convolution_convert_fusion
  248.1 1.7 add_convert_fusion
  (12 shorter events, 0.1 us)
Async XLA Ops:
  6.5 115.3 %copy-start = (bf16[2048,256]{1,0:T(8,128)(2,1)S(1)}, bf16[2048,256]{1,0:T(8,128)(2,1)}, u32[]{:S(2)}) copy-start(bf16[2048,256]{1,0:T(8,128)(2,1)} %param.11) | copy-start | bytes 3145732
  6.5 100.7 %copy-start.5 = (f32[2048]{0:T(1024)S(1)}, f32[2048]{0:T(1024)}, u32[]{:S(2)}) copy-start(f32[2048]{0:T(1024)} %param.10) | copy-start | bytes 24580
  6.5 97.6 %all-gather.4.cloned.1.call-start = ((), (), s32[]{:S(2)}) async-start(), calls=%async_computation.2 | async-start | bytes 5283840 | tf_op jit(solution)/shard_map/all_gather | solution.py:12
  107.3 2.9 %copy-start.4 = (bf16[2048,64]{0,1:T(8,128)(2,1)S(1)}, bf16[2048,64]{0,1:T(8,128)(2,1)}, u32[]{:S(2)}) copy-start(bf16[2048,64]{0,1:T(8,128)(2,1)} %param.13) | copy-start | bytes 786436
  110.2 2.8 %copy-start.1 = (bf16[1024,2048]{1,0:T(8,128)(2,1)}, bf16[1024,2048]{1,0:T(8,128)(2,1)S(1)}, u32[]{:S(2)}) copy-start(bf16[1024,2048]{1,0:T(8,128)(2,1)S(1)} %fusion.2) | copy-start | bytes 12582916
  110.2 1.4 copy-start.3
  113.0 8.8 %copy-start.6 = (s32[8]{0:T(128)S(1)}, s32[8]{0:T(128)}, u32[]{:S(2)}) copy-start(s32[8]{0:T(128)} %param.15) | copy-start | bytes 100
  117.4 30.2 %all-to-all-start = ((bf16[4,2052,64]{1,2,0:T(8,128)(2,1)}), bf16[4,2052,64]{1,2,0:T(8,128)(2,1)S(1)}, u32[]{:S(2)}, u32[]{:S(2)}) async-start(bf16[4,2052,64]{1,2,0:T(8,128)(2,1)} %broadcast_in_dim.24), calls=%async_computation | async-start | bytes 2228224 | tf_op jit(solution)/shard_map/all_to_all | solution.py:27
  121.0 108.6 %all-gather.6.cloned.1.call-start = ((), (), s32[]{:S(2)}) async-start(), calls=%async_computation.3 | async-start | bytes 5242880 | tf_op jit(solution)/shard_map/all_gather | solution.py:141
  224.8 18.9 %all-to-all-start.1 = ((bf16[4,256,256]{1,2,0:T(8,128)(2,1)}), bf16[4,256,256]{1,2,0:T(8,128)(2,1)S(1)}, u32[]{:S(2)}, u32[]{:S(2)}) async-start(bf16[4,256,256]{1,2,0:T(8,128)(2,1)} %copy.42), calls=%async_computation.1 | async-start | bytes 1048576 | tf_op jit(solution)/shard_map/all_to_all | solution.py:140
  243.7 3.5 %copy-start.2 = (bf16[1024,2048]{1,0:T(8,128)(2,1)S(1)}, bf16[1024,2048]{1,0:T(8,128)(2,1)}, u32[]{:S(2)}) copy-start(bf16[1024,2048]{1,0:T(8,128)(2,1)} %all-gather.6.cloned.1.call-done) | copy-start | bytes 12582916
Sparse Core Ops, SparseCore 0:
  9.4 94.6 all-gather.3
  123.9 93.5 all-gather.5
where the time goes:
time: 257 us
  waiting for transfers between devices  131 us (51%)
  blocking collectives  65.6 us (26%)
  other arithmetic  15.3 us (6%)
  matrix products  15 us (6%)
  between operations  13.7 us (5%)
  starting transfers between devices  8.3 us (3%)
  local copies, waits for them, and re-layouts  7.31 us (3%)
    all_gather x1, waiting for transfers between devices, in_one_piece(): filled, at, outs = (lax.all_gather(both, axis, axis=dim, tiled=True), 0, [])  95.2 us
    all_gather x1, blocking collectives, in_one_piece(): filled, at, outs = (lax.all_gather(both, axis, axis=dim, tiled=True), 0, [])  65.6 us
    all_to_all x1, waiting for transfers between devices, from_everyone(): return lax.all_to_all(copies, axis, split_axis=0, concat_axis=0, tiled=True)  21.3 us
    all_to_all x1, waiting for transfers between devices, body(): lax.all_to_all(head_rows, 'tensor', split_axis=0, concat_axis=1, tiled=True)  14.1 us
  transfers between devices with their start and end apart: 4, of which 3 were waited for; matrix products, arithmetic and copies ran while one was open for 6% of the time, Pallas kernels for 0%

commit v1 on v0

--- a/solution.py
+++ b/solution.py
@@ -137,7 +137,15 @@
     head_rows = jnp.where(live_rows[..., None], summed / divisor[..., None], 0.0)
     head_rows = head_rows.reshape(cand_count * cand_len, head_size).astype(jnp.bfloat16)
     row_count = head_rows.shape[0] // tensor_size
-    all_heads = lax.all_to_all(head_rows, "tensor", split_axis=0, concat_axis=1, tiled=True)
+    all_heads = jnp.concatenate(
+        lax.all_to_all(
+            jnp.stack(jnp.split(head_rows, lax.axis_size("tensor"), 0), axis=0),
+            axis_name="tensor",
+            concat_axis=0,
+            split_axis=0,
+        ),
+        1,
+    )
     full_out = lax.all_gather(w_out, "tensor", axis=0, tiled=True)
     summed_out = jnp.zeros((row_count, full_out.shape[1]), jnp.float32)
     for head_index in range(tensor_size):

time: 257 us -> 258 us (level)
  no operation moved by 1% of the time
where the time goes in v1:
time: 258 us; the launch traced here: 257 us
  waiting for transfers between devices  131 us (51%)
  blocking collectives  65.6 us (25%)
  other arithmetic  16.2 us (6%)
  matrix products  15 us (6%)
  between operations  13.8 us (5%)
  starting transfers between devices  8.3 us (3%)
  local copies, waits for them, and re-layouts  6.74 us (3%)
    all_gather x1, waiting for transfers between devices, in_one_piece(): filled, at, outs = (lax.all_gather(both, axis, axis=dim, tiled=True), 0, [])  95.2 us
    all_gather x1, blocking collectives, in_one_piece(): filled, at, outs = (lax.all_gather(both, axis, axis=dim, tiled=True), 0, [])  65.6 us
    all_to_all x1, waiting for transfers between devices, from_everyone(): return lax.all_to_all(copies, axis, split_axis=0, concat_axis=0, tiled=True)  21.3 us
    all_to_all x1, waiting for transfers between devices, body(): lax.all_to_all(jnp.stack(jnp.split(head_rows, lax.axis_size('tensor'), 0)...  14.1 us
  transfers between devices with their start and end apart: 4, of which 3 were waited for; matrix products, arithmetic and copies ran while one was open for 6% of the time, Pallas kernels for 0%

profile of v1, /device:TPU:1, one launch (start us, length us, event | category | flops | bytes accessed | tf_op | source)
XLA Modules:
  0.0 257.0 jit_solution(9171372898754829038)
XLA Ops:
  6.5 0.0 copy-start
  6.5 0.0 all-gather.4.cloned.1.call-start
  6.5 2.4 pad_maximum_fusion
  8.9 0.0 all-gather.4.cloned.1.call-update
  8.9 95.2 %all-gather.4.cloned.1.call-done = bf16[1026,2048]{1,0:T(8,128)(2,1)} async-done(((bf16[1026,512]{1,0:T(8,128)(2,1)}), bf16[1026,2048]{1,0:T(8,128)(2,1)}) %all-gather.4.cloned.1.call-update) | async-done | bytes 4202512 | tf_op jit(solution)/shard_map/all_gather | solution.py:12
  104.2 3.1 %fusion = f32[1024]{0:T(1024)S(1)} fusion(bf16[1026,2048]{1,0:T(8,128)(2,1)} %all-gather.4.cloned.1.call-done), kind=kLoop, calls=%fused_computation.2 | loop fusion | flops 6290432 | bytes 4198400 | tf_op jit(solution)/shard_map/reduce_sum | solution.py:62
  107.2 0.0 copy-done.5
  107.3 0.0 copy-start.4
  107.3 2.9 %fusion.2 = bf16[1024,2048]{1,0:T(8,128)(2,1)S(1)} fusion(f32[2048]{0:T(1024)S(1)} %copy-done.5, f32[1024]{0:T(1024)S(1)} %add_rsqrt_fusion, bf16[1026,2048]{1,0:T(8,128)(2,1)} %all-gather.4.cloned.1.call-done), kind=kLoop, calls=%fused_computation.4 | loop fusion | flops 8388608 | bytes 8400896 | tf_op jit(solution)/shard_map/convert_element_type | solution.py:63
  110.2 0.0 copy-done.4
  110.2 0.0 copy-start.1
  110.2 0.0 copy-start.3
  110.2 1.4 convolution_convert_fusion.4
  111.6 0.0 copy-done.3
  111.6 1.4 convolution_convert_fusion.5
  113.0 0.0 copy-done.1
  113.0 0.0 copy-start.6
  113.0 0.9 fusion.42
  113.9 1.0 convolution_convert_fusion.7
  114.9 0.1 copy.39
  115.0 1.0 convolution_convert_fusion.6
  116.0 0.1 copy.40
  116.2 0.1 concatenate.33
  116.3 1.2 broadcast_in_dim.24
  117.4 3.5 %all-to-all-start = ((bf16[4,2052,64]{1,2,0:T(8,128)(2,1)}), bf16[4,2052,64]{1,2,0:T(8,128)(2,1)S(1)}, u32[]{:S(2)}, u32[]{:S(2)}) async-start(bf16[4,2052,64]{1,2,0:T(8,128)(2,1)} %broadcast_in_dim.24), calls=%async_computation | async-start | bytes 2228224 | tf_op jit(solution)/shard_map/all_to_all | solution.py:27
  121.0 0.0 all-gather.6.cloned.1.call-start
  121.0 0.7 all-gather.6.cloned.1.call-update
  121.8 0.0 copy-done.6
  121.8 0.1 iota_compare_fusion.1
  121.9 0.0 copy-done
  121.9 4.4 %fusion.69 = f32[1024,256]{1,0:T(8,128)} fusion(bf16[1024,2048]{1,0:T(8,128)(2,1)} %copy-done.1, bf16[2048,256]{1,0:T(8,128)(2,1)S(1)} %copy-done), kind=kOutput, calls=%fused_computation.102 | convolution fusion | flops 1073741824 | bytes 6291456 | tf_op jit(solution)/shard_map/dot_general | solution.py:96
  126.3 21.3 %all-to-all-done = bf16[4,2052,64]{1,2,0:T(8,128)(2,1)S(1)} async-done(((bf16[4,2052,64]{1,2,0:T(8,128)(2,1)}), bf16[4,2052,64]{1,2,0:T(8,128)(2,1)S(1)}, u32[]{:S(2)}, u32[]{:S(2)}) %all-to-all-start) | async-done | bytes 1050656 | tf_op jit(solution)/shard_map/all_to_all | solution.py:27
  147.6 1.0 fusion.62
  148.6 0.1 bitcast_convert_fusion
  148.7 0.9 fusion.64
  149.6 0.2 copy.53
  149.8 1.2 copy.54
  151.0 0.1 fusion.63
  151.2 0.1 copy.55
  151.2 0.1 copy.56
  151.3 0.1 copy.47
  151.4 0.1 fusion.54
  151.6 65.6 %all-gather = bf16[32,2,512]{2,1,0:T(2,128)(2,1)S(1)} all-gather(bf16[1,2,512]{2,1,0:T(2,128)(2,1)S(1)} %maximum_bitcast_fusion), channel_id=1, replica_groups=mesh['query'=4,'cand'=32,'tensor'=4] {'cand'}, dimensions={0}, use_global_device_ids=true | all-gather | bytes 67584 | tf_op jit(solution)/shard_map/all_gather | solution.py:12
  217.2 1.1 copy.57
  218.4 3.8 %fusion.22 = (bf16[1024,128]{1,0:T(8,128)(2,1)S(1)}, bf16[1024,128]{1,0:T(8,128)(2,1)S(1)}, f32[1024,128]{1,0:T(8,128)S(1)}, f32[1024,128]{1,0:T(8,128)S(1)}) fusion(f32[1024,128]{1,0:T(8,128)S(1)} %copy.54, f32[1024,128]{1,0:T(8,128)S(1)} %copy.53, f32[128]{0:T(128)S(1)} %multiply_power_fusion, f32[1024]{0:T(1024)S(1)} %convert_bitcast_fusion, ...), kind=kLoop, calls=%fused_computation.40 | loop fusion | flops 1966080 | bytes 3674624 | tf_op jit(solution)/shard_map/convert.7
  222.2 0.3 fusion.68
  222.5 0.3 fusion.67
  222.8 0.1 fusion.33
  222.9 0.1 fusion.29
  223.0 0.4 convolution_multiply_fusion
  223.3 0.4 fusion.5
  223.8 0.1 copy.48
  223.9 0.1 copy.49
  224.1 0.1 copy.50
  224.2 0.1 copy.51
  224.3 0.9 pad_maximum_fusion.1
  225.1 4.7 %all-to-all-start.1 = ((bf16[4,256,256]{1,2,0:T(8,128)(2,1)}), bf16[4,256,256]{1,2,0:T(8,128)(2,1)S(1)}, u32[]{:S(2)}, u32[]{:S(2)}) async-start(bf16[4,256,256]{1,2,0:T(8,128)(2,1)} %pad_maximum_fusion.1), calls=%async_computation.1 | async-start | bytes 1048576 | tf_op jit(solution)/shard_map/all_to_all | solution.py:141
  229.9 14.1 %all-to-all-done.1 = bf16[4,256,256]{1,2,0:T(8,128)(2,1)S(1)} async-done(((bf16[4,256,256]{1,2,0:T(8,128)(2,1)}), bf16[4,256,256]{1,2,0:T(8,128)(2,1)S(1)}, u32[]{:S(2)}, u32[]{:S(2)}) %all-to-all-start.1) | async-done | bytes 524320 | tf_op jit(solution)/shard_map/all_to_all | solution.py:141
  244.0 1.8 convolution_convert_fusion.3
  245.8 1.7 convolution_convert_fusion.2
  247.5 0.0 copy-done.2
  247.5 0.5 convolution_convert_fusion.1
  248.0 0.5 convolution_convert_fusion
  248.5 1.7 add_convert_fusion
  (16 shorter events, 0.2 us)
Async XLA Ops:
  6.5 115.3 %copy-start = (bf16[2048,256]{1,0:T(8,128)(2,1)S(1)}, bf16[2048,256]{1,0:T(8,128)(2,1)}, u32[]{:S(2)}) copy-start(bf16[2048,256]{1,0:T(8,128)(2,1)} %param.11) | copy-start | bytes 3145732
  6.5 100.7 %copy-start.5 = (f32[2048]{0:T(1024)S(1)}, f32[2048]{0:T(1024)}, u32[]{:S(2)}) copy-start(f32[2048]{0:T(1024)} %param.10) | copy-start | bytes 24580
  6.5 97.6 %all-gather.4.cloned.1.call-start = ((), (), s32[]{:S(2)}) async-start(), calls=%async_computation.2 | async-start | bytes 5283840 | tf_op jit(solution)/shard_map/all_gather | solution.py:12
  107.3 2.9 %copy-start.4 = (bf16[2048,64]{0,1:T(8,128)(2,1)S(1)}, bf16[2048,64]{0,1:T(8,128)(2,1)}, u32[]{:S(2)}) copy-start(bf16[2048,64]{0,1:T(8,128)(2,1)} %param.13) | copy-start | bytes 786436
  110.2 2.8 %copy-start.1 = (bf16[1024,2048]{1,0:T(8,128)(2,1)}, bf16[1024,2048]{1,0:T(8,128)(2,1)S(1)}, u32[]{:S(2)}) copy-start(bf16[1024,2048]{1,0:T(8,128)(2,1)S(1)} %fusion.2) | copy-start | bytes 12582916
  110.2 1.4 copy-start.3
  113.0 8.8 %copy-start.6 = (s32[8]{0:T(128)S(1)}, s32[8]{0:T(128)}, u32[]{:S(2)}) copy-start(s32[8]{0:T(128)} %param.15) | copy-start | bytes 100
  117.4 30.2 %all-to-all-start = ((bf16[4,2052,64]{1,2,0:T(8,128)(2,1)}), bf16[4,2052,64]{1,2,0:T(8,128)(2,1)S(1)}, u32[]{:S(2)}, u32[]{:S(2)}) async-start(bf16[4,2052,64]{1,2,0:T(8,128)(2,1)} %broadcast_in_dim.24), calls=%async_computation | async-start | bytes 2228224 | tf_op jit(solution)/shard_map/all_to_all | solution.py:27
  121.0 108.9 %all-gather.6.cloned.1.call-start = ((), (), s32[]{:S(2)}) async-start(), calls=%async_computation.3 | async-start | bytes 5242880 | tf_op jit(solution)/shard_map/all_gather | solution.py:149
  225.1 18.9 %all-to-all-start.1 = ((bf16[4,256,256]{1,2,0:T(8,128)(2,1)}), bf16[4,256,256]{1,2,0:T(8,128)(2,1)S(1)}, u32[]{:S(2)}, u32[]{:S(2)}) async-start(bf16[4,256,256]{1,2,0:T(8,128)(2,1)} %pad_maximum_fusion.1), calls=%async_computation.1 | async-start | bytes 1048576 | tf_op jit(solution)/shard_map/all_to_all | solution.py:141
  244.0 3.5 %copy-start.2 = (bf16[1024,2048]{1,0:T(8,128)(2,1)S(1)}, bf16[1024,2048]{1,0:T(8,128)(2,1)}, u32[]{:S(2)}) copy-start(bf16[1024,2048]{1,0:T(8,128)(2,1)} %all-gather.6.cloned.1.call-done) | copy-start | bytes 12582916
Sparse Core Ops, SparseCore 0:
  9.4 94.6 all-gather.3
  123.9 93.5 all-gather.5
